TPU v7x, 32 devices: a whole 2x2x4 slice. The times are simulated.
32 devices in a mesh: frames: 2 (over core), pix: 16 (over z, y, x).
Axes of the slice: x: 2, y: 2, z: 4, core: 2. Of those that a mesh axis runs over, the one named last changes fastest.
Arguments:
- frames: float32 [256, 32768], P('frames', 'pix'), may hold values from -6 to 6
Outputs:
- sketch: float32 [128, 32768], P(None, 'pix')
- projected: float32 [256, 32768], P('frames', 'pix')
All inputs are finite; a program needn't handle non-finite values.
Results may differ from a plain program's by a relative error of at most 0.0003.
Values sent between devices are 32-bit elements; how exact they have to be, the bound alone decides.
No kernel may reach another device: no remote copies, remote signals or barrier semaphores. Data moves between devices by JAX's collectives and lax.ppermute only.
A program may use at most 64 MiB of HBM per device.

v0:
```python
import jax
import jax.numpy as jnp
from jax import lax
from jax.sharding import PartitionSpec as P


def partner(block, axis, bit):
    count = lax.axis_size(axis)
    route = []
    for low in range(count):
        high = low | 1 << bit
        if high != low and high < count:
            route += [(low, high), (high, low)]
    return lax.ppermute(block, axis, route)


def hdot(left, right):
    return jnp.dot(left, right, precision=lax.Precision.HIGHEST, preferred_element_type=jnp.float32)


def lower_solve(factor, rhs):
    return lax.linalg.triangular_solve(factor, rhs, left_side=True, lower=True)


def rotation(stacked_gram):
    kept = stacked_gram.shape[0] // 2
    subspace = jnp.eye(2 * kept, kept, dtype=jnp.float32)
    product = hdot(stacked_gram, subspace)
    factor = jnp.linalg.cholesky(hdot(product.T, product))
    subspace = lower_solve(factor, product.T).T
    reduced = hdot(subspace.T, hdot(stacked_gram, subspace))
    root_factor = jnp.linalg.cholesky(reduced)
    delta = jnp.trace(reduced) / kept
    damped = jnp.linalg.cholesky(reduced + delta * jnp.eye(kept, dtype=jnp.float32))
    shrunk = lower_solve(damped, reduced)
    whitened = lower_solve(root_factor, subspace.T)
    mixing = hdot(shrunk.T, whitened)
    return (mixing, hdot(shrunk.T, shrunk))


def merge_pair(lower_rows, lower_gram, upper_rows, upper_gram):
    kept = lower_rows.shape[0]
    cross = lax.psum(hdot(lower_rows, upper_rows.T), "pix")
    stacked_gram = jnp.concatenate(
        [
            jnp.concatenate([lower_gram, cross], axis=1),
            jnp.concatenate([cross.T, upper_gram], axis=1),
        ],
        axis=0,
    )
    mixing, new_gram = rotation(stacked_gram)
    merged = hdot(mixing[:, :kept], lower_rows) + hdot(mixing[:, kept:], upper_rows)
    return (merged, new_gram)


def local(frames):
    kept = frames.shape[0]
    sketch = frames
    sketch_gram = lax.psum(hdot(frames, frames.T), "pix")
    position = lax.axis_index("frames")
    span = 1 << 0
    other_rows, other_gram = partner((sketch, sketch_gram), "frames", 0)
    is_upper = position // span % 2 == 1
    lower_rows = jnp.where(is_upper, other_rows, sketch)
    upper_rows = jnp.where(is_upper, sketch, other_rows)
    lower_gram = jnp.where(is_upper, other_gram, sketch_gram)
    upper_gram = jnp.where(is_upper, sketch_gram, other_gram)
    sketch, sketch_gram = merge_pair(lower_rows, lower_gram, upper_rows, upper_gram)
    coeffs = lax.psum(hdot(frames, sketch.T), "pix")
    scaling = 4.0 * kept / (jnp.trace(sketch_gram) + 1e-06)
    projected = hdot(coeffs, sketch) * scaling
    return (sketch, projected)


def solution(mesh):
    return jax.shard_map(
        local,
        mesh=mesh,
        in_specs=(P("frames", "pix"),),
        out_specs=(P(None, "pix"), P("frames", "pix")),
        check_vma=False,
    )
```

profile of v0, /device:TPU:0, one launch (start us, length us, event | category | flops | bytes accessed | tf_op | source)
XLA Modules:
  0.0 313.8 jit_solution(5493166250150651193)
XLA Ops:
  7.2 0.0 all-reduce.6.cloned.1.call-start
  7.2 0.6 collective-permute-start.1
  7.8 0.0 copy-start
  7.8 3.3 %fusion.28 = f32[128,128]{1,0:T(8,128)} fusion(f32[128,2048]{1,0:T(8,128)} %param.4), kind=kOutput, calls=%fused_computation.51 | convolution fusion | flops 402653184 | bytes 1114112 | tf_op jit(solution)/shard_map/dot_general | solution.py:18
  11.0 0.0 collective-permute-done.1
  11.0 0.0 copy-done
  11.0 1.7 fusion.1
  12.7 0.0 all-reduce.6.cloned.1.call-update
  12.8 0.0 all-reduce.4.cloned.1.call-start
  12.8 109.9 %all-reduce.6.cloned.1.call-done = (f32[128,128]{1,0:T(8,128)}, f32[128,128]{1,0:T(8,128)}) async-done(((f32[128,128]{1,0:T(8,128)}, f32[128,128]{1,0:T(8,128)}), (f32[128,128]{1,0:T(8,128)}, f32[128,128]{1,0:T(8,128)})) %all-reduce.6.cloned.1.call-update) | async-done | bytes 131088 | tf_op jit(solution)/shard_map/psum | solution.py:59
  122.7 0.0 collective-permute-start
  122.7 0.0 copy-start.3
  122.7 1.0 copy.3
  123.7 0.0 copy-start.2
  123.7 0.5 collective-permute-done
  124.2 0.0 copy-done.3
  124.2 0.3 copy-done.2
  124.6 0.3 fusion.4
  124.8 0.4 fusion.29
  125.2 0.1 copy.4
  125.3 11.7 %cholesky.59 = f32[128,128]{1,0:T(8,128)S(1)} custom-call(f32[128,128]{1,0:T(8,128)S(1)} %fusion.19), custom_call_target="Cholesky" | custom-call | tf_op jit(solution)/shard_map/jit(cholesky)/cholesky | solution.py:29
  137.1 0.6 compare_reduce_fusion.2
  137.7 0.7 fusion.7
  138.4 9.8 %custom-call.10 = f32[1,128,128]{1,2,0:T(8,128)S(1)} custom-call(f32[1,128,128]{2,1,0:T(8,128)S(1)} %fusion.7), custom_call_target="InvertDiagBlocksLowerTriangular" | custom-call | tf_op jit(solution)/shard_map/triangular_solve/custom-call.0 | solution.py:22
  148.2 0.3 fusion.5
  148.5 0.4 fusion.3
  148.9 0.9 fusion.24
  149.8 0.1 copy.7
  150.5 11.7 %cholesky.81 = f32[128,128]{1,0:T(8,128)S(1)} custom-call(f32[128,128]{1,0:T(8,128)S(1)} %get-tuple-element.8), custom_call_target="Cholesky" | custom-call | tf_op jit(solution)/shard_map/jit(cholesky)/cholesky | solution.py:32
  162.3 0.6 compare_reduce_fusion
  162.9 0.7 fusion.9
  163.6 9.9 %custom-call.11 = f32[1,128,128]{1,2,0:T(8,128)S(1)} custom-call(f32[1,128,128]{2,1,0:T(8,128)S(1)} %fusion.9), custom_call_target="InvertDiagBlocksLowerTriangular" | custom-call | tf_op jit(solution)/shard_map/triangular_solve/custom-call.0 | solution.py:22
  173.5 0.3 fusion.12
  173.9 0.1 copy.5
  174.0 0.1 copy.6
  174.1 11.7 %cholesky.70 = f32[128,128]{1,0:T(8,128)S(1)} custom-call(f32[128,128]{1,0:T(8,128)S(1)} %copy.6), custom_call_target="Cholesky" | custom-call | tf_op jit(solution)/shard_map/jit(cholesky)/cholesky | solution.py:34
  185.8 0.6 compare_reduce_fusion.1
  186.5 0.7 fusion.8
  187.1 9.8 %custom-call.8 = f32[1,128,128]{1,2,0:T(8,128)S(1)} custom-call(f32[1,128,128]{2,1,0:T(8,128)S(1)} %fusion.8), custom_call_target="InvertDiagBlocksLowerTriangular" | custom-call | tf_op jit(solution)/shard_map/triangular_solve | solution.py:22
  196.9 0.3 fusion.15
  197.2 0.3 fusion.30
  197.6 1.0 fusion.2
  198.6 1.0 convolution_add_fusion
  199.6 0.0 copy-start.1
  199.6 1.6 convolution_bitcast_fusion
  201.2 0.0 all-reduce.4.cloned.1.call-update
  201.2 0.9 fusion
  202.8 101.3 %all-reduce.4.cloned.1.call-done = f32[128,128]{0,1:T(8,128)} async-done(((f32[128,128]{0,1:T(8,128)}), f32[128,128]{0,1:T(8,128)}) %all-reduce.4.cloned.1.call-update) | async-done | bytes 65552 | tf_op jit(solution)/shard_map/psum | solution.py:69
  304.1 0.0 copy-done.1
  304.1 2.9 convolution_multiply_fusion
  (7 shorter events, 0.2 us)
Async XLA Ops:
  7.2 115.6 %all-reduce.6.cloned.1.call-start = ((), (), s32[]{:S(2)}) async-start(), calls=%async_computation.1 | async-start | bytes 262144 | tf_op jit(solution)/shard_map/psum | solution.py:59
  7.2 3.8 %collective-permute-start.1 = (f32[128,2048]{1,0:T(8,128)}, f32[128,2048]{1,0:T(8,128)S(1)}, u32[]{:S(2)}, u32[]{:S(2)}) collective-permute-start(f32[128,2048]{1,0:T(8,128)} %param.4), channel_id=1, source_target_pairs={{0,16},{16,0},{1,17},{17,1},{2,18},{18,2},{3,19},{19,3},{4,20},{20... | collective-permute-start | bytes 3145736 | tf_op jit(solution)/shard_map/ppermute | solution.py:14
  7.8 3.3 %copy-start = (f32[128,2048]{1,0:T(8,128)S(1)}, f32[128,2048]{1,0:T(8,128)}, u32[]{:S(2)}) copy-start(f32[128,2048]{1,0:T(8,128)} %param.4) | copy-start | bytes 3145732
  12.8 291.3 %all-reduce.4.cloned.1.call-start = ((), (), s32[]{:S(2)}) async-start(), calls=%async_computation | async-start | bytes 131072 | tf_op jit(solution)/shard_map/psum | solution.py:69
  122.7 1.5 collective-permute-start
  122.7 1.5 copy-start.3
  123.7 0.8 copy-start.2
  199.6 104.5 %copy-start.1 = (f32[128,2048]{1,0:T(8,128)}, f32[128,2048]{1,0:T(8,128)S(1)}, u32[]{:S(2)}) copy-start(f32[128,2048]{1,0:T(8,128)S(1)} %convolution_add_fusion) | copy-start | bytes 3145732
Sparse Core Ops, SparseCore 0:
  14.1 108.6 all-reduce.5
  201.4 102.6 all-reduce.3
where the time goes:
time: 314 us
  waiting for transfers between devices  212 us (68%)
  other arithmetic  68.7 us (22%)
  matrix products  15.5 us (5%)
  between operations  15.5 us (5%)
    psum x1, waiting for transfers between devices, local(): sketch_gram = lax.psum(hdot(frames, frames.T), 'pix')  110 us
    psum x1, waiting for transfers between devices, local(): coeffs = lax.psum(hdot(frames, sketch.T), 'pix')  101 us
    another operation x6, other arithmetic, lower_solve(): return lax.linalg.triangular_solve(factor, rhs, left_side=True, lower=True)  31.5 us
    dot_general x12, matrix products, hdot(): jnp.dot(left, right, precision=lax.Precision.HIGHEST, preferred_element_t...  14.6 us
    another operation x3, other arithmetic, rotation(): jnp.linalg.cholesky(reduced + delta * jnp.eye(kept, dtype=jnp.float32))  12.4 us
    another operation x3, other arithmetic, rotation(): root_factor = jnp.linalg.cholesky(reduced)  12.4 us
    another operation x3, other arithmetic, rotation(): factor = jnp.linalg.cholesky(hdot(product.T, product))  12.4 us
  transfers between devices with their start and end apart: 4, of which 3 were waited for; matrix products, arithmetic and copies ran while one was open for 2% of the time, Pallas kernels for 0%

commit v1 on v0

--- a/solution.py
+++ b/solution.py
@@ -66,7 +66,8 @@
     lower_gram = jnp.where(is_upper, other_gram, sketch_gram)
     upper_gram = jnp.where(is_upper, sketch_gram, other_gram)
     sketch, sketch_gram = merge_pair(lower_rows, lower_gram, upper_rows, upper_gram)
-    coeffs = lax.psum(hdot(frames, sketch.T), "pix")
+    x_in = hdot(frames, sketch.T)
+    coeffs = jnp.sum(lax.all_gather(x_in, "pix"), axis=0)
     scaling = 4.0 * kept / (jnp.trace(sketch_gram) + 1e-06)
     projected = hdot(coeffs, sketch) * scaling
     return (sketch, projected)

time: 314 us -> 266 us (0.85)
  waiting for transfers between devices: 212 us -> 163 us
    psum x1 -> x0, waiting for transfers between devices: 101 us -> none  [local(): coeffs = lax.psum(hdot(frames, sketch.T), 'pix')]
    all_gather x0 -> x1, waiting for transfers between devices: none -> 52.6 us  [local(): coeffs = jnp.sum(lax.all_gather(x_in, 'pix'), axis=0)]
where the time goes in v1:
time: 266 us
  waiting for transfers between devices  163 us (61%)
  other arithmetic  68.9 us (26%)
  between operations  15.7 us (6%)
  matrix products  15 us (6%)
  local copies, waits for them, and re-layouts  3.07 us (1%)
    psum x1, waiting for transfers between devices, local(): sketch_gram = lax.psum(hdot(frames, frames.T), 'pix')  110 us
    all_gather x1, waiting for transfers between devices, local(): coeffs = jnp.sum(lax.all_gather(x_in, 'pix'), axis=0)  52.6 us
    another operation x6, other arithmetic, lower_solve(): return lax.linalg.triangular_solve(factor, rhs, left_side=True, lower=True)  31.5 us
    dot_general x12, matrix products, hdot(): jnp.dot(left, right, precision=lax.Precision.HIGHEST, preferred_element_t...  14.1 us
    another operation x3, other arithmetic, rotation(): jnp.linalg.cholesky(reduced + delta * jnp.eye(kept, dtype=jnp.float32))  12.4 us
    another operation x3, other arithmetic, rotation(): root_factor = jnp.linalg.cholesky(reduced)  12.4 us
    another operation x3, other arithmetic, rotation(): factor = jnp.linalg.cholesky(hdot(product.T, product))  12.4 us
  transfers between devices with their start and end apart: 4, of which 3 were waited for; matrix products, arithmetic and copies ran while one was open for 2% of the time, Pallas kernels for 0%

profile of v1, /device:TPU:0, one launch (start us, length us, event | category | flops | bytes accessed | tf_op | source)
XLA Modules:
  0.0 266.1 jit_solution(17558048553783118469)
XLA Ops:
  7.2 0.0 all-reduce.3.cloned.1.call-start
  7.2 0.6 collective-permute-start.1
  7.8 0.0 copy-start
  7.8 3.5 %fusion.28 = f32[128,128]{1,0:T(8,128)} fusion(f32[128,2048]{1,0:T(8,128)} %param.4), kind=kOutput, calls=%fused_computation.52 | convolution fusion | flops 402653184 | bytes 1114112 | tf_op jit(solution)/shard_map/dot_general | solution.py:18
  11.3 0.0 collective-permute-done.1
  11.3 0.0 copy-done
  11.3 1.7 fusion.1
  13.0 0.0 all-reduce.3.cloned.1.call-update
  13.0 0.0 all-gather.3.cloned.1.call-start
  13.1 109.7 %all-reduce.3.cloned.1.call-done = (f32[128,128]{1,0:T(8,128)}, f32[128,128]{1,0:T(8,128)}) async-done(((f32[128,128]{1,0:T(8,128)}, f32[128,128]{1,0:T(8,128)}), (f32[128,128]{1,0:T(8,128)}, f32[128,128]{1,0:T(8,128)})) %all-reduce.3.cloned.1.call-update) | async-done | bytes 131088 | tf_op jit(solution)/shard_map/psum | solution.py:59
  122.7 0.0 collective-permute-start
  122.7 0.0 copy-start.3
  122.7 1.0 copy.8
  123.7 0.0 copy-start.2
  123.7 0.5 collective-permute-done
  124.2 0.0 copy-done.3
  124.2 0.3 copy-done.2
  124.6 0.3 fusion.4
  124.8 0.4 fusion.29
  125.2 0.1 copy.9
  125.3 11.7 %cholesky.59 = f32[128,128]{1,0:T(8,128)S(1)} custom-call(f32[128,128]{1,0:T(8,128)S(1)} %fusion.19), custom_call_target="Cholesky" | custom-call | tf_op jit(solution)/shard_map/jit(cholesky)/cholesky | solution.py:29
  137.1 0.6 compare_reduce_fusion.2
  137.7 0.7 fusion.7
  138.4 9.8 %custom-call.10 = f32[1,128,128]{1,2,0:T(8,128)S(1)} custom-call(f32[1,128,128]{2,1,0:T(8,128)S(1)} %fusion.7), custom_call_target="InvertDiagBlocksLowerTriangular" | custom-call | tf_op jit(solution)/shard_map/triangular_solve/custom-call.0 | solution.py:22
  148.2 0.3 fusion.5
  148.5 0.4 fusion.3
  148.9 0.9 fusion.24
  149.8 0.1 copy.12
  150.5 11.7 %cholesky.81 = f32[128,128]{1,0:T(8,128)S(1)} custom-call(f32[128,128]{1,0:T(8,128)S(1)} %get-tuple-element.8), custom_call_target="Cholesky" | custom-call | tf_op jit(solution)/shard_map/jit(cholesky)/cholesky | solution.py:32
  162.3 0.6 compare_reduce_fusion
  162.9 0.7 fusion.9
  163.6 9.9 %custom-call.11 = f32[1,128,128]{1,2,0:T(8,128)S(1)} custom-call(f32[1,128,128]{2,1,0:T(8,128)S(1)} %fusion.9), custom_call_target="InvertDiagBlocksLowerTriangular" | custom-call | tf_op jit(solution)/shard_map/triangular_solve/custom-call.0 | solution.py:22
  173.5 0.3 fusion.12
  173.9 0.1 copy.10
  174.0 0.1 copy.11
  174.1 11.7 %cholesky.70 = f32[128,128]{1,0:T(8,128)S(1)} custom-call(f32[128,128]{1,0:T(8,128)S(1)} %copy.11), custom_call_target="Cholesky" | custom-call | tf_op jit(solution)/shard_map/jit(cholesky)/cholesky | solution.py:34
  185.8 0.6 compare_reduce_fusion.1
  186.5 0.7 fusion.8
  187.1 9.8 %custom-call.8 = f32[1,128,128]{1,2,0:T(8,128)S(1)} custom-call(f32[1,128,128]{2,1,0:T(8,128)S(1)} %fusion.8), custom_call_target="InvertDiagBlocksLowerTriangular" | custom-call | tf_op jit(solution)/shard_map/triangular_solve | solution.py:22
  196.9 0.3 fusion.15
  197.2 0.3 fusion.30
  197.6 1.0 fusion.2
  198.6 1.0 convolution_add_fusion
  199.6 0.0 copy-start.1
  199.6 1.6 convolution_bitcast_fusion
  201.2 0.0 all-gather.3.cloned.1.call-update
  201.3 1.0 fusion
  203.0 52.6 %all-gather.3.cloned.1.call-done = f32[2048,128]{0,1:T(8,128)} async-done(((f32[128,128]{0,1:T(8,128)}), f32[2048,128]{0,1:T(8,128)}) %all-gather.3.cloned.1.call-update) | async-done | bytes 1048592 | tf_op jit(solution)/shard_map/all_gather | solution.py:70
  255.6 1.4 copy.13
  257.0 0.2 bitcast_reduce_fusion
  257.2 0.0 copy-done.1
  257.2 2.0 convolution_multiply_fusion
  (7 shorter events, 0.2 us)
Async XLA Ops:
  7.2 115.6 %all-reduce.3.cloned.1.call-start = ((), (), s32[]{:S(2)}) async-start(), calls=%async_computation.1 | async-start | bytes 262144 | tf_op jit(solution)/shard_map/psum | solution.py:59
  7.2 4.1 %collective-permute-start.1 = (f32[128,2048]{1,0:T(8,128)}, f32[128,2048]{1,0:T(8,128)S(1)}, u32[]{:S(2)}, u32[]{:S(2)}) collective-permute-start(f32[128,2048]{1,0:T(8,128)} %param.4), channel_id=1, source_target_pairs={{0,16},{16,0},{1,17},{17,1},{2,18},{18,2},{3,19},{19,3},{4,20},{20... | collective-permute-start | bytes 3145736 | tf_op jit(solution)/shard_map/ppermute | solution.py:14
  7.8 3.5 %copy-start = (f32[128,2048]{1,0:T(8,128)S(1)}, f32[128,2048]{1,0:T(8,128)}, u32[]{:S(2)}) copy-start(f32[128,2048]{1,0:T(8,128)} %param.4) | copy-start | bytes 3145732
  13.0 242.6 %all-gather.3.cloned.1.call-start = ((), (), s32[]{:S(2)}) async-start(), calls=%async_computation | async-start | bytes 1114112 | tf_op jit(solution)/shard_map/all_gather | solution.py:70
  122.7 1.5 collective-permute-start
  122.7 1.5 copy-start.3
  123.7 0.8 copy-start.2
  199.6 57.6 %copy-start.1 = (f32[128,2048]{1,0:T(8,128)}, f32[128,2048]{1,0:T(8,128)S(1)}, u32[]{:S(2)}) copy-start(f32[128,2048]{1,0:T(8,128)S(1)} %convolution_add_fusion) | copy-start | bytes 3145732
Sparse Core Ops, SparseCore 0:
  14.1 108.6 all-reduce.2
  201.4 54.1 all-gather.2
